TPU v7x, 32 devices: a whole 2x2x4 slice. The times are simulated.
32 devices in a mesh: plane: 4 (over y, x), tile: 8 (over z, core).
Axes of the slice: x: 2, y: 2, z: 4, core: 2. Of those that a mesh axis runs over, the one named last changes fastest.
Arguments:
- visibility: float32 [2, 65536], P(None, ('plane', 'tile')), may hold values from -6 to 6
- target: int32 [65536, 1], P(('plane', 'tile')), may hold values from 0 to 31; in each aligned block of 2048 rows (0 to 2047, 2048 to 4095, ...) at most 128 rows name the same one
- offset: int32 [65536], P(('plane', 'tile')), may hold values from 0 to 2097151
- taps: float32 [8], replicated, may hold values from 0.1 to 1
- w_plane: float32 [4], P('plane'), may hold values from -300 to 300
Outputs:
- dirty_image: float32 [4096, 4096], P('plane', 'tile')
Inputs may be any that keep to these rules, and one draw needn't show every extreme that they name: `target`: among the rows of one device no value occurs more than 128 times, and some value occurs exactly 128 times.
All inputs are finite; a program needn't handle non-finite values.
Results may differ from a plain program's by a relative error of at most 0.0042.
Values sent between devices are 32-bit elements; how exact they have to be, the bound alone decides.
A program may use at most 128 MiB of HBM per device.

v0:
```python
import math

import jax
import jax.numpy as jnp
from jax import lax
from jax.sharding import PartitionSpec as P

G = 4096


HIGHEST = lax.Precision.HIGHEST


def shifted(x, axis, by):
    length = lax.axis_size(axis)
    return lax.ppermute(x, axis, [(i, (i + by) % length) for i in range(length)])


def direction(index, length):
    return ((index + length // 2) % length - length // 2).astype(jnp.float32) * (0.5 / length)


def angle_table(first, second, length):
    product = (
        jnp.arange(first, dtype=jnp.int32)[:, None]
        * jnp.arange(second, dtype=jnp.int32)[None, :]
        % length
    )
    angles = product.astype(jnp.float32) * (2.0 * math.pi / length)
    return (jnp.cos(angles), jnp.sin(angles))


def split_length(length):
    inner_len = math.gcd(length, 128)
    return (length // inner_len, inner_len)


def transform_last(real_part, imag_part):
    length = real_part.shape[-1]
    outer_len, inner_len = split_length(length)
    real_grid = real_part.reshape(-1, outer_len, inner_len)
    imag_grid = imag_part.reshape(-1, outer_len, inner_len)
    cos_one, sin_one = angle_table(outer_len, outer_len, outer_len)
    first_re = jnp.einsum("rab,ak->rkb", real_grid, cos_one, precision=HIGHEST) - jnp.einsum(
        "rab,ak->rkb", imag_grid, sin_one, precision=HIGHEST
    )
    first_im = jnp.einsum("rab,ak->rkb", real_grid, sin_one, precision=HIGHEST) + jnp.einsum(
        "rab,ak->rkb", imag_grid, cos_one, precision=HIGHEST
    )
    cos_tw, sin_tw = angle_table(outer_len, inner_len, length)
    twist_re = first_re * cos_tw - first_im * sin_tw
    twist_im = first_re * sin_tw + first_im * cos_tw
    cos_two, sin_two = angle_table(inner_len, inner_len, inner_len)
    out_re = jnp.einsum("rkb,bq->rqk", twist_re, cos_two, precision=HIGHEST) - jnp.einsum(
        "rkb,bq->rqk", twist_im, sin_two, precision=HIGHEST
    )
    out_im = jnp.einsum("rkb,bq->rqk", twist_re, sin_two, precision=HIGHEST) + jnp.einsum(
        "rkb,bq->rqk", twist_im, cos_two, precision=HIGHEST
    )
    return (out_re.reshape(-1, length), out_im.reshape(-1, length))


def transform_first(real_part, imag_part):
    length = real_part.shape[0]
    outer_len, inner_len = split_length(length)
    real_grid = real_part.reshape(outer_len, inner_len, -1)
    imag_grid = imag_part.reshape(outer_len, inner_len, -1)
    cos_one, sin_one = angle_table(outer_len, outer_len, outer_len)
    first_re = jnp.einsum("abc,ak->kbc", real_grid, cos_one, precision=HIGHEST) - jnp.einsum(
        "abc,ak->kbc", imag_grid, sin_one, precision=HIGHEST
    )
    first_im = jnp.einsum("abc,ak->kbc", real_grid, sin_one, precision=HIGHEST) + jnp.einsum(
        "abc,ak->kbc", imag_grid, cos_one, precision=HIGHEST
    )
    cos_tw, sin_tw = angle_table(outer_len, inner_len, length)
    twist_re = first_re * cos_tw[:, :, None] - first_im * sin_tw[:, :, None]
    twist_im = first_re * sin_tw[:, :, None] + first_im * cos_tw[:, :, None]
    cos_two, sin_two = angle_table(inner_len, inner_len, inner_len)
    out_re = jnp.einsum("kbc,bq->qkc", twist_re, cos_two, precision=HIGHEST) - jnp.einsum(
        "kbc,bq->qkc", twist_im, sin_two, precision=HIGHEST
    )
    out_im = jnp.einsum("kbc,bq->qkc", twist_re, sin_two, precision=HIGHEST) + jnp.einsum(
        "kbc,bq->qkc", twist_im, cos_two, precision=HIGHEST
    )
    return (out_re.reshape(length, -1), out_im.reshape(length, -1))


def grid_block(received, taps, start, block_len, band_rows, totals):
    piece = lax.dynamic_slice_in_dim(received, start, block_len, 1)
    encoded = jnp.maximum(piece[2].astype(jnp.int32) - 1, 0)
    band_row = encoded // G
    column = encoded % G
    kernel_len = taps.shape[0]
    taps_low = taps.astype(jnp.bfloat16)
    weight_re = (taps[None, :] * piece[0][:, None]).astype(jnp.bfloat16)
    weight_im = (taps[None, :] * piece[1][:, None]).astype(jnp.bfloat16)
    rel_row = jnp.arange(band_rows, dtype=jnp.int32)[None, :] - band_row[:, None]
    rel_col = (jnp.arange(G, dtype=jnp.int32)[None, :] - column[:, None]) % G
    row_re = jnp.zeros((block_len, band_rows), jnp.bfloat16)
    row_im = jnp.zeros((block_len, band_rows), jnp.bfloat16)
    col_table = jnp.zeros((block_len, G), jnp.bfloat16)
    for tap_index in range(kernel_len):
        row_re = jnp.where(rel_row == tap_index, weight_re[:, tap_index : tap_index + 1], row_re)
        row_im = jnp.where(rel_row == tap_index, weight_im[:, tap_index : tap_index + 1], row_im)
        col_table = jnp.where(rel_col == tap_index, taps_low[tap_index], col_table)
    row_table = jnp.concatenate([row_re, row_im], axis=1)
    return totals + lax.dot_general(
        row_table, col_table, (((0,), (0,)), ((), ())), preferred_element_type=jnp.float32
    )


def local(visibility, target, offset, taps, w_plane):
    tiles = lax.axis_size("tile")
    planes = lax.axis_size("plane")
    devices = tiles * planes
    vis_dev = visibility.shape[1]
    capacity = 2 * vis_dev // devices
    slot_total = devices * capacity
    band = G // tiles
    columns = G // tiles
    kernel_len = taps.shape[0]
    band_rows = band + kernel_len - 1
    destination = target[:, 0]
    onehot = (destination[:, None] == jnp.arange(devices, dtype=jnp.int32)[None, :]).astype(
        jnp.int32
    )
    rank = jnp.sum(jnp.cumsum(onehot, axis=0) * onehot, axis=1) - 1
    slot = destination * capacity + rank
    payload = jnp.stack([visibility[0], visibility[1], offset.astype(jnp.float32) + 1.0])
    outgoing = jnp.zeros((3, slot_total), jnp.float32).at[:, slot].set(payload)
    received = lax.all_to_all(outgoing, ("plane", "tile"), split_axis=1, concat_axis=1, tiled=True)
    block_len = min(512, slot_total)
    empty = jnp.zeros((2 * band_rows, G), jnp.float32)

    def grid_step(index, totals):
        return grid_block(received, taps, index * block_len, block_len, band_rows, totals)

    gridded = lax.fori_loop(0, slot_total // block_len, grid_step, empty)
    gridded = gridded.reshape(2, band_rows, G)
    incoming = shifted(gridded[:, band:], "tile", 1)
    grid_band = gridded[:, :band].at[:, : kernel_len - 1].add(incoming)
    col_re, col_im = transform_last(grid_band[0], grid_band[1])
    stacked = jnp.stack([col_re, col_im]).reshape(2, band, tiles, columns)
    exchanged = lax.all_to_all(stacked, "tile", split_axis=2, concat_axis=1, tiled=True)
    item_count = exchanged.shape[3]
    rows_re, rows_im = transform_first(
        exchanged[0].reshape(G, item_count), exchanged[1].reshape(G, item_count)
    )
    image_parts = jnp.stack([rows_re, rows_im]).reshape(2, G, 1, item_count).reshape(2, G, columns)
    line_pos = jnp.arange(G, dtype=jnp.int32)
    column_pos = lax.axis_index("tile") * columns + jnp.arange(columns, dtype=jnp.int32)
    cos_row = direction(line_pos, G)
    cos_col = direction(column_pos, G)
    n_minus = (
        jnp.sqrt(1.0 - cos_row[:, None] * cos_row[:, None] - cos_col[None, :] * cos_col[None, :])
        - 1.0
    )
    phase = 2.0 * math.pi * w_plane[0] * n_minus
    screened = jnp.cos(phase) * image_parts[0] - jnp.sin(phase) * image_parts[1]
    summed = lax.psum_scatter(screened, "plane", scatter_dimension=0, tiled=True)
    return summed * (1.0 / math.sqrt(vis_dev * devices))


def solution(mesh):
    return jax.shard_map(
        local,
        mesh=mesh,
        in_specs=(
            P(None, ("plane", "tile")),
            P(("plane", "tile"), None),
            P(("plane", "tile")),
            P(),
            P("plane"),
        ),
        out_specs=P("plane", "tile"),
        check_vma=False,
    )
```

profile of v0, /device:TPU:0, one launch (start us, length us, event | category | flops | bytes accessed | tf_op | source)
XLA Modules:
  0.0 1112.9 jit_solution(1792978015275601666)
XLA Ops:
  42.5 216.9 %while.18 = (s32[]{:T(128)}, f32[1038,4096]{1,0:T(8,128)}, f32[3,4096]{1,0:T(4,128)S(1)}, f32[8]{0:T(128)}, bf16[8]{0:T(256)(128)(2,1)S(1)}, /*index=5*/s32[]{:T...) while((s32[]{:T(128)}, f32[1038,4096]{1,0:T(8,128)}, f32[3,4096]{1,0:T(4,128)S(1)}, ...), condition=%wide.region_5.6_spmd.clone, body=%wide.region_4.5_spmd.clone.sunk | while | flops 4429704192 | bytes 36240668 | solution.py:138
  46.1 20.6 %select_add_fusion.2 = f32[1038,4096]{1,0:T(8,128)} fusion(f32[1038,4096]{1,0:T(8,128)} %get-tuple-element.356, pred[]{:T(512)S(6)} %compare.38, s32[512]{0:T(512)S(1)} %get-tuple-element.312, bf16[]{:T(256)} %bitcast.127, bf16[]{:T(256)} %bitcast.128, bf16[]{:T(256)} %bitcast.129, bf16[]{:T(256)} %bitcast.130, bf16[]{:T(256)} %bitcast.131, ...), kind=kOutput, calls=%fused_computation.1.clone.1 | convolution fusion | flops 4423036928 | bytes 35078160 | tf_op jit(solution)/shard_map/while/body/eval_jaxpr/dot_general | solution.py:107
  70.2 23.9 %select_add_fusion.2 = f32[1038,4096]{1,0:T(8,128)} fusion(f32[1038,4096]{1,0:T(8,128)} %get-tuple-element.356, pred[]{:T(512)S(6)} %compare.38, s32[512]{0:T(512)S(1)} %get-tuple-element.312, bf16[]{:T(256)} %bitcast.127, bf16[]{:T(256)} %bitcast.128, bf16[]{:T(256)} %bitcast.129, bf16[]{:T(256)} %bitcast.130, bf16[]{:T(256)} %bitcast.131, ...), kind=kOutput, calls=%fused_computation.1.clone.1 | convolution fusion | flops 4423036928 | bytes 35078160 | tf_op jit(solution)/shard_map/while/body/eval_jaxpr/dot_general | solution.py:107
  97.7 23.9 %select_add_fusion.2 = f32[1038,4096]{1,0:T(8,128)} fusion(f32[1038,4096]{1,0:T(8,128)} %get-tuple-element.356, pred[]{:T(512)S(6)} %compare.38, s32[512]{0:T(512)S(1)} %get-tuple-element.312, bf16[]{:T(256)} %bitcast.127, bf16[]{:T(256)} %bitcast.128, bf16[]{:T(256)} %bitcast.129, bf16[]{:T(256)} %bitcast.130, bf16[]{:T(256)} %bitcast.131, ...), kind=kOutput, calls=%fused_computation.1.clone.1 | convolution fusion | flops 4423036928 | bytes 35078160 | tf_op jit(solution)/shard_map/while/body/eval_jaxpr/dot_general | solution.py:107
  125.3 23.9 %select_add_fusion.2 = f32[1038,4096]{1,0:T(8,128)} fusion(f32[1038,4096]{1,0:T(8,128)} %get-tuple-element.356, pred[]{:T(512)S(6)} %compare.38, s32[512]{0:T(512)S(1)} %get-tuple-element.312, bf16[]{:T(256)} %bitcast.127, bf16[]{:T(256)} %bitcast.128, bf16[]{:T(256)} %bitcast.129, bf16[]{:T(256)} %bitcast.130, bf16[]{:T(256)} %bitcast.131, ...), kind=kOutput, calls=%fused_computation.1.clone.1 | convolution fusion | flops 4423036928 | bytes 35078160 | tf_op jit(solution)/shard_map/while/body/eval_jaxpr/dot_general | solution.py:107
  152.8 23.9 %select_add_fusion.2 = f32[1038,4096]{1,0:T(8,128)} fusion(f32[1038,4096]{1,0:T(8,128)} %get-tuple-element.356, pred[]{:T(512)S(6)} %compare.38, s32[512]{0:T(512)S(1)} %get-tuple-element.312, bf16[]{:T(256)} %bitcast.127, bf16[]{:T(256)} %bitcast.128, bf16[]{:T(256)} %bitcast.129, bf16[]{:T(256)} %bitcast.130, bf16[]{:T(256)} %bitcast.131, ...), kind=kOutput, calls=%fused_computation.1.clone.1 | convolution fusion | flops 4423036928 | bytes 35078160 | tf_op jit(solution)/shard_map/while/body/eval_jaxpr/dot_general | solution.py:107
  180.4 23.9 %select_add_fusion.2 = f32[1038,4096]{1,0:T(8,128)} fusion(f32[1038,4096]{1,0:T(8,128)} %get-tuple-element.356, pred[]{:T(512)S(6)} %compare.38, s32[512]{0:T(512)S(1)} %get-tuple-element.312, bf16[]{:T(256)} %bitcast.127, bf16[]{:T(256)} %bitcast.128, bf16[]{:T(256)} %bitcast.129, bf16[]{:T(256)} %bitcast.130, bf16[]{:T(256)} %bitcast.131, ...), kind=kOutput, calls=%fused_computation.1.clone.1 | convolution fusion | flops 4423036928 | bytes 35078160 | tf_op jit(solution)/shard_map/while/body/eval_jaxpr/dot_general | solution.py:107
  207.9 23.9 %select_add_fusion.2 = f32[1038,4096]{1,0:T(8,128)} fusion(f32[1038,4096]{1,0:T(8,128)} %get-tuple-element.356, pred[]{:T(512)S(6)} %compare.38, s32[512]{0:T(512)S(1)} %get-tuple-element.312, bf16[]{:T(256)} %bitcast.127, bf16[]{:T(256)} %bitcast.128, bf16[]{:T(256)} %bitcast.129, bf16[]{:T(256)} %bitcast.130, bf16[]{:T(256)} %bitcast.131, ...), kind=kOutput, calls=%fused_computation.1.clone.1 | convolution fusion | flops 4423036928 | bytes 35078160 | tf_op jit(solution)/shard_map/while/body/eval_jaxpr/dot_general | solution.py:107
  235.4 23.9 %select_add_fusion.2 = f32[1038,4096]{1,0:T(8,128)} fusion(f32[1038,4096]{1,0:T(8,128)} %get-tuple-element.356, pred[]{:T(512)S(6)} %compare.38, s32[512]{0:T(512)S(1)} %get-tuple-element.312, bf16[]{:T(256)} %bitcast.127, bf16[]{:T(256)} %bitcast.128, bf16[]{:T(256)} %bitcast.129, bf16[]{:T(256)} %bitcast.130, bf16[]{:T(256)} %bitcast.131, ...), kind=kOutput, calls=%fused_computation.1.clone.1 | convolution fusion | flops 4423036928 | bytes 35078160 | tf_op jit(solution)/shard_map/while/body/eval_jaxpr/dot_general | solution.py:107
  334.3 19.1 %subtract_bitcast_fusion.1 = (f32[512,32,128]{2,1,0:T(8,128)}, f32[512,32,128]{2,1,0:T(8,128)}) fusion(f32[32,128]{1,0:T(8,128)S(1)} %get-tuple-element.239, f32[32,128]{1,0:T(8,128)S(1)} %get-tuple-element.240, f32[32,512,128]{2,0,1:T(8,128)} %fusion.143, f32[32,512,128]{2,0,1:T(8,128)} %fusion.149, f32[32,512,128]{2,0,1:T(8,128)} %fusion.145, ...), kind=kOutput, calls=%fused_computation.116 | convolution fusion | flops 822097920 | bytes 50364416 | tf_op jit(solution)/shard_map/rab,ak->rkb/dot_general | solution.py:44
  353.4 21.6 %fusion.84 = f32[128,512,32]{1,0,2:T(8,128)} fusion(f32[512,32,128]{2,1,0:T(8,128)} %get-tuple-element.234), kind=kOutput, calls=%fused_computation.135 | convolution fusion | flops 3221454848 | bytes 16777216 | tf_op jit(solution)/shard_map/rkb,bq->rqk/dot_general | solution.py:54
  375.0 16.1 %fusion.82 = f32[128,512,32]{1,0,2:T(8,128)S(1)} fusion(f32[512,32,128]{2,1,0:T(8,128)S(1)} %copy-done.2), kind=kOutput, calls=%fused_computation.133 | convolution fusion | flops 3221454848 | bytes 16777216 | tf_op jit(solution)/shard_map/rkb,bq->rqk/dot_general | solution.py:57
  391.1 15.9 %subtract_bitcast_fusion = f32[512,128,32]{0,1,2:T(8,128)} fusion(f32[128,512,32]{1,0,2:T(8,128)} %fusion.84, f32[512,32,128]{2,1,0:T(8,128)S(1)} %bitcast.140), kind=kOutput, calls=%fused_computation.114 | convolution fusion | flops 3223552000 | bytes 25165824 | tf_op jit(solution)/shard_map/rkb,bq->rqk/dot_general | solution.py:54
  418.5 13.7 %add_bitcast_fusion = f32[512,128,32]{0,1,2:T(8,128)} fusion(f32[128,512,32]{1,0,2:T(8,128)S(1)} %fusion.82, f32[512,32,128]{2,1,0:T(8,128)S(1)} %bitcast.140), kind=kOutput, calls=%fused_computation.113 | convolution fusion | flops 3223552000 | bytes 25165824 | tf_op jit(solution)/shard_map/rkb,bq->rqk/dot_general | solution.py:57
  455.4 362.7 %all-to-all-done.1 = f32[2,512,8,512]{1,3,0,2:T(8,128)} async-done(((f32[2,512,8,512]{1,3,0,2:T(8,128)}), f32[2,512,8,512]{1,3,0,2:T(8,128)}, u32[]{:S(2)}, u32[]{:S(2)}) %all-to-all-start.1) | async-done | bytes 16777248 | tf_op jit(solution)/shard_map/all_to_all | solution.py:144
  818.1 17.6 %copy.53 = f32[2,512,8,512]{3,1,2,0:T(8,128)} copy(f32[2,512,8,512]{1,3,0,2:T(8,128)} %all-to-all-done.1) | data formatting | bytes 33554432 | tf_op jit(solution)/shard_map/all_to_all | solution.py:144
  855.8 13.4 %fusion.76 = f32[32,128,512]{2,0,1:T(8,128)} fusion(f32[32,128,512]{2,1,0:T(8,128)S(1)} %bitcast.146), kind=kOutput, calls=%fused_computation.127 | convolution fusion | flops 805320704 | bytes 16777216 | tf_op jit(solution)/shard_map/abc,ak->kbc/dot_general | solution.py:69
  882.4 24.2 %multiply_subtract_fusion = (f32[32,128,512]{2,0,1:T(8,128)}, f32[32,128,512]{2,0,1:T(8,128)}) fusion(f32[32,128]{0,1:T(8,128)S(1)} %copy.59, f32[32,128]{0,1:T(8,128)S(1)} %copy.56, f32[32,128,512]{2,0,1:T(8,128)} %fusion.74, f32[32,128,512]{2,0,1:T(8,128)} %fusion.80, f32[32,128,512]{2,0,1:T(8,128)} %fusion.76, f32[32,128,512]{2,1,0:T(8,128)} %bitcast.148), kind=kOutput, calls=%fused_computation.112 | convolution fusion | flops 822097920 | bytes 50364416 | tf_op jit(solution)/shard_map/abc,ak->kbc/dot_general | solution.py:72
  906.7 17.0 %fusion.68 = f32[128,32,512]{2,0,1:T(8,128)S(1)} fusion(f32[32,128,512]{2,0,1:T(8,128)} %get-tuple-element.232), kind=kOutput, calls=%fused_computation.119 | convolution fusion | flops 3221454848 | bytes 16777216 | tf_op jit(solution)/shard_map/kbc,bq->qkc/dot_general | solution.py:79
  923.7 13.6 %fusion.66 = f32[128,32,512]{2,0,1:T(8,128)} fusion(f32[32,128,512]{2,0,1:T(8,128)S(1)} %copy-done), kind=kOutput, calls=%fused_computation.117 | convolution fusion | flops 3221454848 | bytes 16777216 | tf_op jit(solution)/shard_map/kbc,bq->qkc/dot_general | solution.py:82
  937.3 13.6 %fusion.94 = f32[128,32,512]{2,0,1:T(8,128)} fusion(f32[128,32,512]{2,0,1:T(8,128)S(1)} %fusion.68, f32[32,128,512]{2,0,1:T(8,128)S(1)} %bitcast.138), kind=kOutput, calls=%fused_computation.141 | convolution fusion | flops 3223552000 | bytes 25165824 | tf_op jit(solution)/shard_map/kbc,bq->qkc/dot_general | solution.py:79
  959.1 15.6 %fusion.97 = f32[128,32,512]{2,0,1:T(8,128)} fusion(f32[128,32,512]{2,0,1:T(8,128)} %fusion.66, f32[32,128,512]{2,0,1:T(8,128)S(1)} %bitcast.138), kind=kOutput, calls=%fused_computation.142 | convolution fusion | flops 3223552000 | bytes 25165824 | tf_op jit(solution)/shard_map/kbc,bq->qkc/dot_general | solution.py:82
  983.0 36.1 %fusion.65 = f32[4096,512]{1,0:T(8,128)} fusion(f32[128,32,512]{2,1,0:T(8,128)S(1)} %copy.65, f32[128,32,512]{2,1,0:T(8,128)S(1)} %copy.62, f32[512]{0:T(512)S(1)} %fusion.178, f32[4096]{0:T(1024)S(1)} %fusion.134, f32[]{:T(128)} %bitcast), kind=kLoop, calls=%fused_computation.109 | loop fusion | flops 12582912 | bytes 25184260 | tf_op jit(solution)/shard_map/sub | solution.py:159
  1019.1 83.6 %reduce-scatter.2.cloned.1.call-done = f32[1024,512]{1,0:T(8,128)} async-done(((f32[4096,512]{1,0:T(8,128)}), f32[1024,512]{1,0:T(8,128)}) %reduce-scatter.2.cloned.1.call-update) | async-done | bytes 2097168 | tf_op jit(solution)/shard_map/reduce_scatter | solution.py:160
  (133 shorter events, 226.2 us)
Async XLA Ops:
  27.7 14.7 %all-to-all-start = ((f32[3,32,128]{2,0,1:T(4,128)}), f32[3,32,128]{2,0,1:T(4,128)S(1)}, u32[]{:S(2)}, u32[]{:S(2)}) async-start(f32[3,32,128]{2,0,1:T(4,128)} %copy.45), calls=%async_computation | async-start | bytes 131072 | tf_op jit(solution)/shard_map/all_to_all | solution.py:131
  273.6 12.0 %collective-permute-start = (f32[2,7,4096]{2,1,0:T(8,128)S(1)}, f32[2,7,4096]{2,1,0:T(8,128)S(1)}, u32[]{:S(2)}, u32[]{:S(2)}) collective-permute-start(f32[2,7,4096]{2,1,0:T(8,128)S(1)} %slice.407), channel_id=1, source_target_pairs={{0,1},{1,2},{2,3},{3,4},{4,5},{5,6},{6,7},{7,0},{8,9},{9,10},{10,1... | collective-permute-start | bytes 688136 | tf_op jit(solution)/shard_map/ppermute | solution.py:16
  324.8 9.5 copy-start.1
  353.4 21.6 %copy-start.2 = (f32[512,32,128]{2,1,0:T(8,128)S(1)}, f32[512,32,128]{2,1,0:T(8,128)}, u32[]{:S(2)}) copy-start(f32[512,32,128]{2,1,0:T(8,128)} %get-tuple-element.234) | copy-start | bytes 25165828
  353.4 37.7 %slice-start.2 = ((s8[8388608]{0:T(1024)(128)(4,1)}), s8[4194304]{0:T(1024)(128)(4,1)S(1)}, s32[]{:S(2)}) async-start(s8[8388608]{0:T(1024)(128)(4,1)} %bitcast.139), calls=%async_computation.6 | async-start | bytes 8388608
  375.0 16.1 %slice-start.3 = ((s8[8388608]{0:T(1024)(128)(4,1)}), s8[4194304]{0:T(1024)(128)(4,1)S(1)}, s32[]{:S(2)}) async-start(s8[8388608]{0:T(1024)(128)(4,1)} %bitcast.139), calls=%async_computation.7 | async-start | bytes 8388608
  432.2 8.4 copy-start.4
  448.7 369.4 %all-to-all-start.1 = ((f32[2,512,8,512]{1,3,0,2:T(8,128)}), f32[2,512,8,512]{1,3,0,2:T(8,128)}, u32[]{:S(2)}, u32[]{:S(2)}) async-start(f32[2,512,8,512]{1,3,0,2:T(8,128)} %copy.52), calls=%async_computation.1 | async-start | bytes 33554432 | tf_op jit(solution)/shard_map/all_to_all | solution.py:144
  454.5 648.2 %reduce-scatter.2.cloned.1.call-start = ((), (), s32[]{:S(2)}) async-start(), calls=%async_computation.3 | async-start | bytes 10485760 | tf_op jit(solution)/shard_map/reduce_scatter | solution.py:160
  842.6 26.7 %copy-start.3 = (f32[1,8,512,1,512]{4,2,1,3,0:T(8,128)}, f32[1,8,512,1,512]{4,2,1,3,0:T(8,128)S(1)}, u32[]{:S(2)}) copy-start(f32[1,8,512,1,512]{4,2,1,3,0:T(8,128)S(1)} %get-tuple-element.236) | copy-start | bytes 25165828
  906.7 17.0 %copy-start = (f32[32,128,512]{2,0,1:T(8,128)S(1)}, f32[32,128,512]{2,0,1:T(8,128)}, u32[]{:S(2)}) copy-start(f32[32,128,512]{2,0,1:T(8,128)} %get-tuple-element.232) | copy-start | bytes 25165828
  906.7 30.6 %slice-start = ((s8[8388608]{0:T(1024)(128)(4,1)}), s8[4194304]{0:T(1024)(128)(4,1)S(1)}, s32[]{:S(2)}) async-start(s8[8388608]{0:T(1024)(128)(4,1)} %bitcast.137), calls=%async_computation.4 | async-start | bytes 8388608
  923.7 13.6 %slice-start.1 = ((s8[8388608]{0:T(1024)(128)(4,1)}), s8[4194304]{0:T(1024)(128)(4,1)S(1)}, s32[]{:S(2)}) async-start(s8[8388608]{0:T(1024)(128)(4,1)} %bitcast.137), calls=%async_computation.5 | async-start | bytes 8388608
Sparse Core Ops, SparseCore 0:
  1019.2 83.4 reduce-scatter.1
where the time goes:
time: 1120 us; the launch traced here: 1110 us
  waiting for transfers between devices  453 us (40%)
  matrix products  427 us (38%)
  local copies, waits for them, and re-layouts  127 us (11%)
  other arithmetic  77.7 us (7%)
  between operations  14.6 us (1%)
  starting transfers between devices  13.5 us (1%)
    all_to_all x1, waiting for transfers between devices, local(): lax.all_to_all(stacked, 'tile', split_axis=2, concat_axis=1, tiled=True)  363 us
    dot_general x8, matrix products, grid_block(): lax.dot_general(row_table, col_table, (((0,), (0,)), ((), ())), preferred...  188 us
    reduce_scatter x1, waiting for transfers between devices, local(): lax.psum_scatter(screened, 'plane', scatter_dimension=0, tiled=True)  83.6 us
    sub x1, other arithmetic, local(): screened = jnp.cos(phase) * image_parts[0] - jnp.sin(phase) * image_parts[1]  36.1 us
    dot_general x1, matrix products, transform_first(): jnp.einsum('abc,ak->kbc', real_grid, sin_one, precision=HIGHEST)  24.2 us
  transfers between devices with their start and end apart: 4, of which 3 were waited for; matrix products, arithmetic and copies ran while one was open for 1% of the time, Pallas kernels for 0%

commit v1 on v0

v1 whole, which is shorter than its diff:
```python
import functools
import math

import jax
import jax.numpy as jnp
import numpy as np
from jax import lax
from jax.experimental import pallas as pl
from jax.experimental.pallas import tpu as pltpu
from jax.sharding import PartitionSpec as P

G = 4096
CHUNK = 256
BASE = 64


def fitted(function, terms):
    nodes = np.cos((np.arange(400) + 0.5) * np.pi / 400)
    square = 0.125 * (nodes + 1.0)
    table = np.polynomial.chebyshev.Chebyshev.fit(
        square, function(np.sqrt(square)), terms - 1, domain=[0.0, 0.25]
    )
    return [float(v) for v in table.convert(kind=np.polynomial.Polynomial).coef]


COS_COEF = fitted(lambda x: np.cos(2.0 * np.pi * x), 7)
SIN_COEF = fitted(lambda x: np.sin(2.0 * np.pi * x) / x, 6)


def horner(coefficients, x):
    total = coefficients[-1]
    for value in coefficients[-2::-1]:
        total = total * x + value
    return total


def turn(cycles):
    part = cycles - jnp.round(cycles)
    square = part * part
    return horner(COS_COEF, square), part * horner(SIN_COEF, square)


def grid_kernel(columns, count_ref, first_ref, vis_ref, out_ref, acc_ref, table_ref):
    tile, step = pl.program_id(0), pl.program_id(1)
    rows = acc_ref.shape[0]

    @pl.when(step == 0)
    def _():
        acc_ref[...] = jnp.zeros_like(acc_ref)

    @pl.when(step * CHUNK < count_ref[tile])
    def _():
        vis_re = vis_ref[0, 0:1, :]
        vis_im = vis_ref[0, 1:2, :]
        encoded = vis_ref[0, 2:3, :] - 1.0
        row = jnp.floor(encoded * (1.0 / G))
        column = encoded - row * G
        unit = column * (1.0 / G)
        place = lax.broadcasted_iota(jnp.int32, (BASE, CHUNK), 0).astype(jnp.float32)
        base_cos, base_sin = turn(place * unit)
        jump = lax.broadcasted_iota(jnp.int32, (8, CHUNK), 0) * BASE + first_ref[0]
        jump_cos, jump_sin = turn(jump.astype(jnp.float32) * unit)
        lead_re = vis_re * jump_cos - vis_im * jump_sin
        lead_im = vis_re * jump_sin + vis_im * jump_cos
        for block in range(columns // BASE):
            one_re = lead_re[block : block + 1]
            one_im = lead_im[block : block + 1]
            start = block * BASE
            table_ref[start : start + BASE] = (base_cos * one_re - base_sin * one_im).astype(
                jnp.bfloat16
            )
            table_ref[columns + start : columns + start + BASE] = (
                base_cos * one_im + base_sin * one_re
            ).astype(jnp.bfloat16)
        lines = lax.broadcasted_iota(jnp.int32, (rows, CHUNK), 0)
        onehot = jnp.where(lines == row.astype(jnp.int32), 1.0, 0.0).astype(jnp.bfloat16)
        acc_ref[...] += lax.dot_general(
            onehot, table_ref[...], (((1,), (1,)), ((), ())), preferred_element_type=jnp.float32
        )

    @pl.when(step == pl.num_programs(1) - 1)
    def _():
        out_ref[0, 0] = acc_ref[:, :columns].astype(out_ref.dtype)
        out_ref[0, 1] = acc_ref[:, columns:].astype(out_ref.dtype)


def image_kernel(
    tiles, weight_ref, w_ref, grid_ref, dft_ref, twist_ref, line_ref, side_ref, out_ref,
    half_ref, mixed_ref, full_ref,
):
    digit = pl.program_id(0)
    rows, columns = grid_ref.shape[2], grid_ref.shape[3]
    half = tiles // 2
    step = 32

    @pl.when(digit == 0)
    def _():
        @pl.loop(0, rows // step)
        def _(index):
            part = pl.ds(pl.multiple_of(index * step, step), step)
            for t in range(half):
                for c in range(2):
                    low = grid_ref[t, c, part, :].astype(jnp.float32)
                    high = grid_ref[t + half, c, part, :].astype(jnp.float32)
                    half_ref[0, t, c, part, :] = low + high
                    half_ref[1, t, c, part, :] = low - high

    parity = lax.rem(digit, 2)

    @pl.loop(0, rows // step)
    def _(index):
        at = pl.multiple_of(index * step, step)
        part = pl.ds(at, step)
        total_re = half_ref[parity, 0, 0, part, :]
        total_im = half_ref[parity, 0, 1, part, :]
        for t in range(1, half):
            cos_t = weight_ref[0, digit * half + t]
            sin_t = weight_ref[1, digit * half + t]
            value_re = half_ref[parity, t, 0, part, :]
            value_im = half_ref[parity, t, 1, part, :]
            total_re = total_re + (value_re * cos_t - value_im * sin_t)
            total_im = total_im + (value_re * sin_t + value_im * cos_t)
        twist_cos = twist_ref[0, part, 0:1]
        twist_sin = twist_ref[0, part, 1:2]
        mixed_ref[part, :] = (total_re * twist_cos - total_im * twist_sin).astype(jnp.bfloat16)
        mixed_ref[pl.ds(rows + at, step), :] = (
            total_re * twist_sin + total_im * twist_cos
        ).astype(jnp.bfloat16)

    full_ref[...] = jnp.dot(dft_ref[...], mixed_ref[...], preferred_element_type=jnp.float32)
    w = w_ref[0]

    @pl.loop(0, rows // step)
    def _(index):
        at = pl.multiple_of(index * step, step)
        part = pl.ds(at, step)
        flat = line_ref[0, part, 0:1]
        line_angle = line_ref[0, part, 1:2]
        line_size = line_ref[0, part, 2:3]
        root = jnp.sqrt(flat - side_ref[0:1, :])
        cycles = w * (root - 1.0) + (line_angle + side_ref[1:2, :])
        cos_s, sin_s = turn(cycles)
        picture = cos_s * full_ref[part, :] - sin_s * full_ref[pl.ds(rows + at, step), :]
        out_ref[part, digit, :] = picture * (
            line_size * side_ref[2:3, :]
        )


def direction(index, length):
    return ((index + length // 2) % length - length // 2).astype(jnp.float32) * (0.5 / length)


def response(taps, index):
    shifts = jnp.arange(taps.shape[0], dtype=jnp.int32)
    angles = (shifts[None, :] * index[:, None] % G).astype(jnp.float32) * (2.0 * math.pi / G)
    real = jnp.sum(jnp.cos(angles) * taps[None, :], axis=1)
    imag = jnp.sum(jnp.sin(angles) * taps[None, :], axis=1)
    return jnp.arctan2(imag, real) * (0.5 / math.pi), jnp.sqrt(real * real + imag * imag)


def local(visibility, target, offset, taps, w_plane):
    tiles = lax.axis_size("tile")
    planes = lax.axis_size("plane")
    devices = tiles * planes
    vis_dev = visibility.shape[1]
    capacity = 2 * vis_dev // devices
    slot_total = devices * capacity
    band = G // tiles
    columns = G // tiles
    destination = target[:, 0]
    onehot = (destination[:, None] == jnp.arange(devices, dtype=jnp.int32)[None, :]).astype(
        jnp.int32
    )
    rank = jnp.sum(jnp.cumsum(onehot, axis=0) * onehot, axis=1) - 1
    slot = destination * capacity + rank
    payload = jnp.stack([visibility[0], visibility[1], offset.astype(jnp.float32) + 1.0])
    outgoing = jnp.zeros((3, slot_total), jnp.float32).at[:, slot].set(payload)
    received = lax.all_to_all(outgoing, ("plane", "tile"), split_axis=1, concat_axis=1, tiled=True)
    used = received[2] > 0.0
    place = jnp.where(used, jnp.cumsum(used.astype(jnp.int32)) - 1, slot_total)
    packed = jnp.zeros((3, slot_total), jnp.float32).at[:, place].set(received, mode="drop")
    gathered = lax.all_gather(packed, "tile", axis=0)
    counts = jnp.sum((gathered[:, 2] > 0.0).astype(jnp.int32), axis=1)
    first = (lax.axis_index("tile") * columns).astype(jnp.int32)
    smem = pl.BlockSpec(memory_space=pltpu.SMEM)
    steps = slot_total // CHUNK
    grids = pl.pallas_call(
        functools.partial(grid_kernel, columns),
        grid=(tiles, steps),
        out_shape=jax.ShapeDtypeStruct((tiles, 2, band, columns), jnp.bfloat16),
        in_specs=[smem, smem, pl.BlockSpec((1, 3, CHUNK), lambda t, k: (t, 0, k))],
        out_specs=pl.BlockSpec((1, 2, band, columns), lambda t, k: (t, 0, 0, 0)),
        scratch_shapes=[
            pltpu.VMEM((band, 2 * columns), jnp.float32),
            pltpu.VMEM((2 * columns, CHUNK), jnp.bfloat16),
        ],
    )(counts, first[None], gathered)

    numbers = np.arange(band)
    angles = 2.0 * np.pi * (numbers[:, None] * numbers[None, :] % band) / band
    cos_d, sin_d = np.cos(angles), np.sin(angles)
    dft = np.block([[cos_d, -sin_d], [sin_d, cos_d]]).astype(jnp.bfloat16)
    digits = np.arange(tiles)
    angles = 2.0 * np.pi * (digits[:, None] * np.arange(tiles // 2)[None, :] % tiles) / tiles
    weights = np.stack([np.cos(angles).ravel(), np.sin(angles).ravel()]).astype(np.float32)
    angles = 2.0 * np.pi * (digits[:, None] * numbers[None, :]) / G
    twist = np.stack([np.cos(angles), np.sin(angles)], axis=2).astype(np.float32)

    line_pos = jnp.arange(G, dtype=jnp.int32)
    line_angle, line_size = response(taps, line_pos)
    cos_row = direction(line_pos, G)
    line = jnp.stack(
        [1.0 - cos_row * cos_row, line_angle, line_size * (1.0 / math.sqrt(vis_dev * devices))],
        axis=1,
    )
    line = line.reshape(band, tiles, 3).transpose(1, 0, 2)
    column_pos = first + jnp.arange(columns, dtype=jnp.int32)
    side_angle, side_size = response(taps.astype(jnp.bfloat16).astype(jnp.float32), column_pos)
    cos_col = direction(column_pos, G)
    side = jnp.stack([cos_col * cos_col, side_angle, side_size])

    screened = pl.pallas_call(
        functools.partial(image_kernel, tiles),
        grid=(tiles,),
        out_shape=jax.ShapeDtypeStruct((band, tiles, columns), jnp.float32),
        in_specs=[
            smem,
            smem,
            pl.BlockSpec((tiles, 2, band, columns), lambda d: (0, 0, 0, 0)),
            pl.BlockSpec((2 * band, 2 * band), lambda d: (0, 0)),
            pl.BlockSpec((1, band, 2), lambda d: (d, 0, 0)),
            pl.BlockSpec((1, band, 3), lambda d: (d, 0, 0)),
            pl.BlockSpec((3, columns), lambda d: (0, 0)),
        ],
        out_specs=pl.BlockSpec((band, tiles, columns), lambda d: (0, 0, 0)),
        scratch_shapes=[
            pltpu.VMEM((2, tiles // 2, 2, band, columns), jnp.float32),
            pltpu.VMEM((2 * band, columns), jnp.bfloat16),
            pltpu.VMEM((2 * band, columns), jnp.float32),
        ],
        compiler_params=pltpu.CompilerParams(vmem_limit_bytes=64 * 1024 * 1024 - 65536),
    )(jnp.asarray(weights), w_plane, grids, jnp.asarray(dft), jnp.asarray(twist), line, side)
    return lax.psum_scatter(screened.reshape(G, columns), "plane", scatter_dimension=0, tiled=True)


def solution(mesh):
    return jax.shard_map(
        local,
        mesh=mesh,
        in_specs=(
            P(None, ("plane", "tile")),
            P(("plane", "tile"), None),
            P(("plane", "tile")),
            P(),
            P("plane"),
        ),
        out_specs=P("plane", "tile"),
        check_vma=False,
    )
```

time: 1120 us -> 307 us (0.27)
  matrix products: 427 us -> 0 us
  waiting for transfers between devices: 453 us -> 89.7 us
  Pallas kernels: 0 us -> 125 us
  local copies, waits for them, and re-layouts: 127 us -> 31.4 us
  other arithmetic: 77.7 us -> 19.7 us
  blocking collectives: 0 us -> 15.2 us
    dot_general x24 -> x0, matrix products: 427 us -> none  [the longest x8 188 us: grid_block(): lax.dot_general(row_table, col_table, (((0,), (0,)), ((), ())), preferred...]
    all_to_all x1 -> x0, waiting for transfers between devices: 363 us -> none  [local(): lax.all_to_all(stacked, 'tile', split_axis=2, concat_axis=1, tiled=True)]
    pallas_call x0 -> x2, Pallas kernels: none -> 125 us  [the longest x1 71.6 us: local(): pl.pallas_call(functools.partial(grid_kernel, columns), grid=(tiles, step...]
    sub x2, other arithmetic: 36.1 us -> 1.31 us  [the longest x1 1.23 us: local(): 1.0 - cos_row * cos_row]
    slice x27 -> x1, local copies, waits for them, and re-layouts: 26.3 us -> 0.13 us  [the longest x1 11.5 us: local(): grid_band = gridded[:, :band].at[:, :kernel_len - 1].add(incoming)]
    sub x2 -> x0, local copies, waits for them, and re-layouts: 19.7 us -> none  [the longest x1 11.5 us: transform_last(): jnp.einsum('rkb,bq->rqk', twist_re, cos_two, precision=HIGHEST)]
    all_to_all x1 -> x0, local copies, waits for them, and re-layouts: 17.6 us -> none  [local(): lax.all_to_all(stacked, 'tile', split_axis=2, concat_axis=1, tiled=True)]
    add x2 -> x0, local copies, waits for them, and re-layouts: 16.6 us -> none  [the longest x1 8.39 us: transform_last(): jnp.einsum('rkb,bq->rqk', twist_re, sin_two, precision=HIGHEST)]
  transfers between devices with their start and end apart: 4 -> 2, of which waited for: 3 -> 1; matrix products, arithmetic and copies ran while one was open for 1% -> 5% of each run, Pallas kernels for 0% -> 0%
where the time goes in v1:
time: 307 us; the launch traced here: 303 us
  Pallas kernels  125 us (41%)
  waiting for transfers between devices  89.7 us (29%)
  local copies, waits for them, and re-layouts  31.4 us (10%)
  other arithmetic  19.7 us (6%)
  blocking collectives  15.2 us (5%)
  between operations  14.2 us (5%)
  starting transfers between devices  7.55 us (2%)
    reduce_scatter x1, waiting for transfers between devices, local(): lax.psum_scatter(screened.reshape(G, columns), 'plane', scatter_dimension...  89.7 us
    pallas_call x1, Pallas kernels, local(): pl.pallas_call(functools.partial(grid_kernel, columns), grid=(tiles, step...  71.6 us
    pallas_call x1, Pallas kernels, local(): pl.pallas_call(functools.partial(image_kernel, tiles), grid=(tiles,), out...  53.9 us
    all_gather x1, blocking collectives, local(): gathered = lax.all_gather(packed, 'tile', axis=0)  15.2 us
    scatter x1, local copies, waits for them, and re-layouts, local(): jnp.zeros((3, slot_total), jnp.float32).at[:, place]  11.4 us
    another operation x5, other arithmetic  9.75 us
    all_to_all x1, starting transfers between devices, local(): lax.all_to_all(outgoing, ('plane', 'tile'), split_axis=1, concat_axis=1,...  7.33 us
  transfers between devices with their start and end apart: 2, of which 1 were waited for; matrix products, arithmetic and copies ran while one was open for 5% of the time, Pallas kernels for 0%

profile of v1, /device:TPU:0, one launch (start us, length us, event | category | flops | bytes accessed | tf_op | source)
XLA Modules:
  0.0 303.2 jit_solution(4493457395784007881)
XLA Ops:
  6.5 0.7 convert_add_fusion
  7.3 0.7 fusion.12
  8.0 9.1 %reduce-window.15 = s32[32,16,128]{2,1,0:T(8,128)S(1)} reduce-window(s32[32,16,128]{2,1,0:T(8,128)S(1)} %fusion.12, s32[]{:T(128)} %constant.47.clone.1), window={size=1x1x128 pad=0_0x0_0x127_0}, to_apply=%region_0.0 | reduce-window | flops 8323072 | bytes 524292 | tf_op jit(solution)/shard_map/reduce-window
  17.2 0.2 copy.55
  18.0 0.4 copy.48
  18.3 6.1 %scatter_custom_fusion = f32[3,4096]{0,1:T(8,128)S(1)} fusion(s32[2048]{0:T(1024)S(1)} %bitcast.57, f32[2048,3]{1,0:T(8,128)S(1)} %copy.48, f32[]{:T(128)} %constant.42.clone.1), kind=kCustom, calls=%fused_computation.14 | custom fusion | bytes 49156 | tf_op jit(solution)/shard_map/scatter | solution.py:177
  24.5 1.2 copy.49
  25.7 7.3 %all-to-all-start = ((f32[3,32,128]{2,0,1:T(4,128)}), f32[3,32,128]{2,0,1:T(4,128)S(1)}, u32[]{:S(2)}, u32[]{:S(2)}) async-start(f32[3,32,128]{2,0,1:T(4,128)} %copy.49), calls=%async_computation | async-start | bytes 131072 | tf_op jit(solution)/shard_map/all_to_all | solution.py:178
  33.0 0.2 reduce-scatter.2.cloned.1.call-start
  33.3 0.6 multiply_reduce_fusion
  33.9 1.2 fusion.5
  36.2 4.4 %copy.54 = f32[512,8,1]{2,0,1:T(8,128)} copy(f32[512,8,1]{1,0,2:T(8,128)S(1)} %mul.253) | data formatting | bytes 32768 | tf_op jit(solution)/shard_map/mul | solution.py:213
  40.6 4.4 %copy.53 = f32[512,8,1]{2,0,1:T(8,128)} copy(f32[512,8,1]{1,0,2:T(8,128)S(1)} %mul.248) | data formatting | bytes 32768 | tf_op jit(solution)/shard_map/mul | solution.py:158
  45.1 4.7 %maximum_bitcast_fusion.line_ref = f32[8,512,3]{2,1,0:T(8,128)} fusion(f32[512,8,1]{2,0,1:T(8,128)} %copy.54, f32[512,8,1]{2,0,1:T(8,128)} %copy.53, f32[512,8,1]{2,0,1:T(8,128)S(1)} %fusion.5), kind=kLoop, calls=%fused_computation.11 | loop fusion | flops 24576 | bytes 98304 | tf_op jit(solution)/shard_map/transpose | solution.py:216
  49.8 0.6 pad_maximum_fusion.side_ref
  50.4 0.3 reduce-window.19
  51.1 2.0 copy.50
  53.1 11.4 %scatter_custom_fusion.1 = f32[3,4096]{0,1:T(8,128)S(1)} fusion(s32[4096]{0:T(1024)S(1)} %bitcast.56, f32[4096,3]{1,0:T(8,128)} %copy.50, f32[]{:T(128)} %constant.42.clone.1), kind=kCustom, calls=%fused_computation.12 | custom fusion | bytes 49664 | tf_op jit(solution)/shard_map/scatter | solution.py:181
  64.5 0.6 copy.51
  65.1 15.2 %all-gather.1.vis_ref = f32[8,3,4096]{2,1,0:T(4,128)S(1)} all-gather(f32[1,3,4096]{2,1,0:T(4,128)S(1)} %copy.51), channel_id=2, replica_groups=mesh['plane'=4,'tile'=8] {'tile'}, dimensions={0}, use_global_device_ids=true | all-gather | bytes 442368 | tf_op jit(solution)/shard_map/all_gather | solution.py:182
  80.4 0.9 fusion.16.count_ref
  81.3 71.6 %shard_map.82.grid_ref = bf16[8,2,512,512]{3,2,1,0:T(8,128)(2,1)} custom-call(s32[8]{0:T(128)} %fusion.16.count_ref, s32[1]{0:T(128)} %bitcast.17.first_ref, f32[8,3,4096]{2,1,0:T(4,128)} %copy-done), custom_call_target="tpu_custom_call" | custom-call | tf_op jit(solution)/shard_map/pallas_call | solution.py:187
  152.8 53.9 %shard_map.83 = f32[512,8,512]{2,1,0:T(8,128)} custom-call(f32[2,32]{1,0:T(2,128)} %constant.97.clone.weight_ref, f32[1]{0:T(128)S(6)} %copy.58.w_ref, bf16[8,2,512,512]{3,2,1,0:T(8,128)(2,1)} %shard_map.82.grid_ref, bf16[1024,1024]{1,0:T(8,128)(2,1)} %constant.98.clone.dft_ref, f32[8,512,2]{2,1,0:T(8,128)} %constant.99.clone.twist_ref, ...), custom_call_target="tpu_custom_call" | custom-call | tf_op jit(solution)/shard_map/pallas_call | solution.py:222
  206.7 89.7 %reduce-scatter.2.cloned.1.call-done = f32[1024,512]{1,0:T(8,128)} async-done(((f32[4096,512]{1,0:T(8,128)}), f32[1024,512]{1,0:T(8,128)}) %reduce-scatter.2.cloned.1.call-update) | async-done | bytes 2097168 | tf_op jit(solution)/shard_map/reduce_scatter | solution.py:243
  (31 shorter events, 1.6 us)
Async XLA Ops:
  6.5 11.2 %copy-start.1 = (s32[2048,1]{0,1:T(1,128)S(1)}, s32[2048,1]{0,1:T(1,128)}, u32[]{:S(2)}) copy-start(s32[2048,1]{0,1:T(1,128)} %param.9) | copy-start | bytes 24580
  6.5 11.4 %copy-start.2 = (f32[2,2048]{1,0:T(2,128)S(1)}, f32[2,2048]{1,0:T(2,128)}, u32[]{:S(2)}) copy-start(f32[2,2048]{1,0:T(2,128)} %param.8) | copy-start | bytes 49156
  18.3 15.0 %copy-start.3 = (f32[8]{0:T(128)S(1)}, f32[8]{0:T(128)}, u32[]{:S(2)}) copy-start(f32[8]{0:T(128)} %param.11) | copy-start | bytes 100
  25.7 24.7 %all-to-all-start = ((f32[3,32,128]{2,0,1:T(4,128)}), f32[3,32,128]{2,0,1:T(4,128)S(1)}, u32[]{:S(2)}, u32[]{:S(2)}) async-start(f32[3,32,128]{2,0,1:T(4,128)} %copy.49), calls=%async_computation | async-start | bytes 131072 | tf_op jit(solution)/shard_map/all_to_all | solution.py:178
  33.0 263.4 %reduce-scatter.2.cloned.1.call-start = ((), (), s32[]{:S(2)}) async-start(), calls=%async_computation.2 | async-start | bytes 10485760 | tf_op jit(solution)/shard_map/reduce_scatter | solution.py:243
  80.4 0.9 copy-start
Sparse Core Ops, SparseCore 0:
  206.8 89.5 reduce-scatter.1
